TPU v7x, 32 devices: a whole 2x2x4 slice. The times are simulated.
32 devices in a mesh: row: 8 (over y, x, core), col: 4 (over z).
Axes of the slice: x: 2, y: 2, z: 4, core: 2. Of those that a mesh axis runs over, the one named last changes fastest.
Arguments:
- history: float32 [3, 512, 4096], P(None, None, ('row', 'col')), may hold values from -8 to 8
Outputs:
- orbitals: float32 [512, 4096], P(None, ('row', 'col'))
All inputs are finite; a program needn't handle non-finite values.
Results may differ from a plain program's by a relative error of at most 0.0003.
Values sent between devices are 32-bit elements; how exact they have to be, the bound alone decides.
A program may use at most 64 MiB of HBM per device.

v0:
```python
import jax
import jax.numpy as jnp
from jax import lax
from jax.sharding import PartitionSpec as P


def on_device(history):
    precise = lax.Precision.HIGHEST
    npw_total = history.shape[2] * lax.axis_size("row") * lax.axis_size("col")
    newest = history[0]
    local_terms = tuple(
        (jnp.einsum("ip,jp->ij", newest, history[index], precision=precise) for index in range(3))
    )
    summed = lax.psum(local_terms, ("row", "col"))
    weights = (2.5, -2.0, 0.5)
    predicted = jnp.zeros(newest.shape, jnp.float32)
    for index in range(3):
        project = summed[index] / npw_total
        predicted = predicted + weights[index] * jnp.dot(project, history[index], precision=precise)
    local_gram = jnp.einsum("ip,jp->ij", predicted, predicted, precision=precise)
    gram = lax.psum(local_gram, ("row", "col"))
    factor = jnp.linalg.cholesky(gram / npw_total)
    return lax.linalg.triangular_solve(factor, predicted, left_side=True, lower=True)


def solution(mesh):
    return jax.shard_map(
        on_device,
        mesh=mesh,
        in_specs=(P(None, None, ("row", "col")),),
        out_specs=P(None, ("row", "col")),
        check_vma=False,
    )
```

profile of v0, /device:TPU:0, one launch (start us, length us, event | category | flops | bytes accessed | tf_op | source)
XLA Modules:
  0.0 441.3 jit_solution(1607792850113480831)
XLA Ops:
  6.5 0.0 copy-start
  6.5 0.0 all-reduce.7.cloned.1.call-start
  6.5 3.1 fusion.11
  9.7 0.0 copy-done
  9.7 2.0 fusion.14
  11.6 2.0 fusion.19
  13.6 0.0 all-reduce.7.cloned.1.call-update
  13.6 0.5 all-reduce.5.cloned.1.call-start
  14.1 141.3 %all-reduce.7.cloned.1.call-done = (f32[512,512]{0,1:T(8,128)}, f32[512,512]{0,1:T(8,128)}, f32[512,512]{0,1:T(8,128)}) async-done(((f32[512,512]{0,1:T(8,128)}, f32[512,512]{0,1:T(8,128)}, f32[512,512]{0,1:T(8,128)}), (f32[512,512]{0,1:T(8,128)}, f32[512,512]{0,1:T(8,128)}, f32[512,512]{0,1:T(8,128)})) %all-reduce.7.cloned.1.call-update) | async-done | bytes 3145744 | tf_op jit(solution)/shard_map/psum | solution.py:14
  155.4 0.0 copy-start.3
  155.4 3.1 convolution_multiply_fusion.2
  158.5 0.0 copy-start.2
  158.6 0.0 copy-done.3
  158.6 1.8 fusion.1
  160.4 0.0 copy-done.2
  160.4 1.8 fusion
  162.2 2.0 fusion.61
  164.3 0.0 all-reduce.5.cloned.1.call-update
  164.3 130.2 %all-reduce.5.cloned.1.call-done = f32[512,512]{0,1:T(8,128)} async-done(((f32[512,512]{0,1:T(8,128)}), f32[512,512]{0,1:T(8,128)}) %all-reduce.5.cloned.1.call-update) | async-done | bytes 1048592 | tf_op jit(solution)/shard_map/psum | solution.py:21
  294.5 1.3 broadcast_multiply_fusion
  295.8 0.0 copy-start.1
  295.8 0.3 copy.3
  296.2 0.9 copy-done.1
  297.0 0.2 fusion.2
  297.3 11.7 %cholesky.104 = f32[128,128]{1,0:T(8,128)S(1)} custom-call(f32[128,128]{1,0:T(8,128)S(1)} %cholesky.266), custom_call_target="Cholesky" | custom-call | tf_op jit(solution)/shard_map/jit(cholesky)/cholesky | solution.py:22
  309.0 10.0 %custom-call.30 = f32[1,128,128]{1,2,0:T(8,128)S(1)} custom-call(f32[1,128,128]{2,1,0:T(8,128)S(1)} %get-tuple-element.35), custom_call_target="InvertDiagBlocksLowerTriangular" | custom-call | tf_op jit(solution)/shard_map/jit(cholesky)/cholesky | solution.py:22
  319.0 0.1 cholesky.224
  319.1 0.3 constant_dynamic-update-slice_fusion.3
  319.4 0.3 convolution_subtract_fusion
  319.8 11.7 %cholesky.217 = f32[128,128]{1,0:T(8,128)S(1)} custom-call(f32[128,128]{1,0:T(8,128)S(1)} %cholesky.270), custom_call_target="Cholesky" | custom-call | tf_op jit(solution)/shard_map/jit(cholesky)/cholesky | solution.py:22
  331.5 9.8 %custom-call.31 = f32[1,128,128]{1,2,0:T(8,128)S(1)} custom-call(f32[1,128,128]{2,1,0:T(8,128)S(1)} %get-tuple-element.32), custom_call_target="InvertDiagBlocksLowerTriangular" | custom-call | tf_op jit(solution)/shard_map/jit(cholesky)/cholesky | solution.py:22
  341.4 0.3 convolution_dynamic-update-slice_fusion
  341.6 0.4 convolution_subtract_fusion.1
  342.0 11.7 %cholesky.238 = f32[128,128]{1,0:T(8,128)S(1)} custom-call(f32[128,128]{1,0:T(8,128)S(1)} %cholesky.275), custom_call_target="Cholesky" | custom-call | tf_op jit(solution)/shard_map/jit(cholesky)/cholesky | solution.py:22
  353.8 0.7 compare_reduce_fusion.1
  354.5 10.0 %custom-call.32 = f32[1,128,128]{1,2,0:T(8,128)S(1)} custom-call(f32[1,128,128]{2,1,0:T(8,128)S(1)} %get-tuple-element.29), custom_call_target="InvertDiagBlocksLowerTriangular" | custom-call | tf_op jit(solution)/shard_map/jit(cholesky)/cholesky | solution.py:22
  364.5 0.2 convolution_dynamic-update-slice_fusion.1
  364.7 0.4 convolution_subtract_fusion.5
  365.1 11.7 %cholesky.255 = f32[128,128]{1,0:T(8,128)S(1)} custom-call(f32[128,128]{1,0:T(8,128)S(1)} %convolution_subtract_fusion.5), custom_call_target="Cholesky" | custom-call | tf_op jit(solution)/shard_map/jit(cholesky)/cholesky | solution.py:22
  376.8 0.6 compare_reduce_fusion
  377.5 0.7 compare_reduce_fusion.2
  380.7 0.1 select_select_fusion
  380.8 10.6 %while.1 = (s32[]{:T(128)}, f32[512,512]{1,0:T(8,128)S(1)}, s32[4,2]{0,1:T(2,128)S(1)}, f32[4,128,128]{2,1,0:T(8,128)}, s32[]{:T(128)}) while((s32[]{:T(128)}, f32[512,512]{1,0:T(8,128)S(1)}, s32[4,2]{0,1:T(2,128)S(1)}, f32[4,128,128]{2,1,0:T(8,128)}, s32[]{:T(128)}) %tuple.27), condition=%wide.while_cond, body=%wide.while_body.sunk | while | flops 2 | bytes 132705 | solution.py:23
  380.9 0.1 constant_dynamic-slice_fusion.2
  380.9 0.6 fusion.70
  381.5 2.0 bitcast_dynamic-update-slice_fusion.2
  383.5 0.1 constant_dynamic-slice_fusion.2
  383.6 0.6 fusion.70
  384.2 2.0 bitcast_dynamic-update-slice_fusion.2
  386.2 0.1 constant_dynamic-slice_fusion.2
  386.2 0.6 fusion.70
  386.8 2.0 bitcast_dynamic-update-slice_fusion.2
  388.8 0.1 constant_dynamic-slice_fusion.2
  388.9 0.6 fusion.70
  389.5 2.0 bitcast_dynamic-update-slice_fusion.2
  391.4 40.1 %custom-call.33 = f32[4,128,128]{1,2,0:T(8,128)S(1)} custom-call(f32[4,128,128]{2,1,0:T(8,128)} %get-tuple-element.12), custom_call_target="InvertDiagBlocksLowerTriangular" | custom-call | tf_op jit(solution)/shard_map/triangular_solve | solution.py:23
  431.6 0.3 fusion.48
  431.9 0.2 convolution_subtract_fusion.3
  432.1 0.3 fusion.47
  432.4 0.3 convolution_subtract_fusion.2
  432.6 0.3 fusion.45
  432.9 0.3 convolution_subtract_fusion.4
  433.3 0.3 fusion.44
  433.5 0.7 pad_maximum_fusion
  (10 shorter events, 0.2 us)
Async XLA Ops:
  6.5 3.1 copy-start
  6.5 148.9 %all-reduce.7.cloned.1.call-start = ((), (), s32[]{:S(2)}) async-start(), calls=%async_computation.1 | async-start | bytes 6291456 | tf_op jit(solution)/shard_map/psum | solution.py:14
  13.6 280.9 %all-reduce.5.cloned.1.call-start = ((), (), s32[]{:S(2)}) async-start(), calls=%async_computation | async-start | bytes 2097152 | tf_op jit(solution)/shard_map/psum | solution.py:21
  155.4 3.1 copy-start.3
  158.5 1.8 copy-start.2
  295.8 1.2 copy-start.1
Sparse Core Ops, SparseCore 0:
  13.8 141.6 all-reduce.6
  164.4 130.0 all-reduce.4
where the time goes:
time: 444 us; the launch traced here: 441 us
  waiting for transfers between devices  271 us (61%)
  other arithmetic  121 us (27%)
  matrix products  19.7 us (4%)
  between operations  16.4 us (4%)
  local copies, waits for them, and re-layouts  11.9 us (3%)
    psum x1, waiting for transfers between devices, on_device(): summed = lax.psum(local_terms, ('row', 'col'))  141 us
    psum x1, waiting for transfers between devices, on_device(): gram = lax.psum(local_gram, ('row', 'col'))  130 us
    another operation x14, other arithmetic, on_device(): factor = jnp.linalg.cholesky(gram / npw_total)  78.8 us
    another operation x4, other arithmetic, on_device(): lax.linalg.triangular_solve(factor, predicted, left_side=True, lower=True)  41 us
    another operation x12, local copies, waits for them, and re-layouts  10.6 us
  transfers between devices with their start and end apart: 2, of which 2 were waited for; matrix products, arithmetic and copies ran while one was open for 0% of the time, Pallas kernels for 0%

commit v1 on v0

--- a/solution.py
+++ b/solution.py
@@ -11,7 +11,7 @@
     local_terms = tuple(
         (jnp.einsum("ip,jp->ij", newest, history[index], precision=precise) for index in range(3))
     )
-    summed = lax.psum(local_terms, ("row", "col"))
+    summed = lax.psum(lax.psum(local_terms, "col"), "row")
     weights = (2.5, -2.0, 0.5)
     predicted = jnp.zeros(newest.shape, jnp.float32)
     for index in range(3):

time: 444 us -> 499 us (1.12)
  waiting for transfers between devices: 271 us -> 326 us
    psum x1 -> x2, waiting for transfers between devices: 141 us -> 195 us  [on_device(): summed = lax.psum(lax.psum(local_terms, 'col'), 'row')]
  transfers between devices with their start and end apart: 2 -> 3, of which waited for: 2 -> 3; matrix products, arithmetic and copies ran while one was open for 0% -> 0% of each run, Pallas kernels for 0% -> 0%
where the time goes in v1:
time: 499 us; the launch traced here: 496 us
  waiting for transfers between devices  326 us (65%)
  other arithmetic  121 us (24%)
  matrix products  19.7 us (4%)
  between operations  16.1 us (3%)
  local copies, waits for them, and re-layouts  11.9 us (2%)
    psum x2, waiting for transfers between devices, on_device(): summed = lax.psum(lax.psum(local_terms, 'col'), 'row')  195 us
    psum x1, waiting for transfers between devices, on_device(): gram = lax.psum(local_gram, ('row', 'col'))  131 us
    another operation x14, other arithmetic, on_device(): factor = jnp.linalg.cholesky(gram / npw_total)  78.8 us
    another operation x4, other arithmetic, on_device(): lax.linalg.triangular_solve(factor, predicted, left_side=True, lower=True)  41 us
    another operation x12, local copies, waits for them, and re-layouts  10.6 us
  transfers between devices with their start and end apart: 3, of which 3 were waited for; matrix products, arithmetic and copies ran while one was open for 0% of the time, Pallas kernels for 0%

profile of v1, /device:TPU:0, one launch (start us, length us, event | category | flops | bytes accessed | tf_op | source)
XLA Modules:
  0.0 496.1 jit_solution(16473956735357557848)
XLA Ops:
  6.5 0.0 all-reduce.11.cloned.1.call-start
  6.5 3.1 fusion.11
  9.7 0.0 copy-done
  9.7 2.0 fusion.14
  11.6 2.0 fusion.19
  13.6 0.0 all-reduce.11.cloned.1.call-update
  13.6 0.0 all-reduce.9.cloned.1.call-start
  13.7 123.9 %all-reduce.11.cloned.1.call-done = (f32[512,512]{0,1:T(8,128)}, f32[512,512]{0,1:T(8,128)}, f32[512,512]{0,1:T(8,128)}) async-done(((f32[512,512]{0,1:T(8,128)}, f32[512,512]{0,1:T(8,128)}, f32[512,512]{0,1:T(8,128)}), (f32[512,512]{0,1:T(8,128)}, f32[512,512]{0,1:T(8,128)}, f32[512,512]{0,1:T(8,128)})) %all-reduce.11.cloned.1.call-update) | async-done | bytes 3145744 | tf_op jit(solution)/shard_map/psum | solution.py:14
  137.6 0.0 all-reduce.9.cloned.1.call-update
  137.6 0.5 all-reduce.7.cloned.1.call-start
  138.1 71.6 %all-reduce.9.cloned.1.call-done = (f32[512,512]{0,1:T(8,128)}, f32[512,512]{0,1:T(8,128)}, f32[512,512]{0,1:T(8,128)}) async-done(((f32[512,512]{0,1:T(8,128)}, f32[512,512]{0,1:T(8,128)}, f32[512,512]{0,1:T(8,128)}), (f32[512,512]{0,1:T(8,128)}, f32[512,512]{0,1:T(8,128)}, f32[512,512]{0,1:T(8,128)})) %all-reduce.9.cloned.1.call-update) | async-done | bytes 3145744 | tf_op jit(solution)/shard_map/psum | solution.py:14
  209.7 3.1 convolution_multiply_fusion.2
  212.8 0.0 copy-start.2
  212.8 0.0 copy-done.3
  212.8 1.8 fusion.1
  214.7 0.0 copy-done.2
  214.7 1.8 fusion
  216.5 2.0 fusion.61
  218.5 0.0 all-reduce.7.cloned.1.call-update
  218.6 131.0 %all-reduce.7.cloned.1.call-done = f32[512,512]{0,1:T(8,128)} async-done(((f32[512,512]{0,1:T(8,128)}), f32[512,512]{0,1:T(8,128)}) %all-reduce.7.cloned.1.call-update) | async-done | bytes 1048592 | tf_op jit(solution)/shard_map/psum | solution.py:21
  349.6 1.3 broadcast_multiply_fusion
  350.9 0.3 copy.3
  351.2 0.9 copy-done.1
  352.1 0.2 fusion.2
  352.4 11.7 %cholesky.104 = f32[128,128]{1,0:T(8,128)S(1)} custom-call(f32[128,128]{1,0:T(8,128)S(1)} %cholesky.266), custom_call_target="Cholesky" | custom-call | tf_op jit(solution)/shard_map/jit(cholesky)/cholesky | solution.py:22
  364.1 10.0 %custom-call.30 = f32[1,128,128]{1,2,0:T(8,128)S(1)} custom-call(f32[1,128,128]{2,1,0:T(8,128)S(1)} %get-tuple-element.38), custom_call_target="InvertDiagBlocksLowerTriangular" | custom-call | tf_op jit(solution)/shard_map/jit(cholesky)/cholesky | solution.py:22
  374.1 0.1 cholesky.224
  374.2 0.3 constant_dynamic-update-slice_fusion.3
  374.5 0.3 convolution_subtract_fusion
  374.9 11.7 %cholesky.217 = f32[128,128]{1,0:T(8,128)S(1)} custom-call(f32[128,128]{1,0:T(8,128)S(1)} %cholesky.270), custom_call_target="Cholesky" | custom-call | tf_op jit(solution)/shard_map/jit(cholesky)/cholesky | solution.py:22
  386.6 9.8 %custom-call.31 = f32[1,128,128]{1,2,0:T(8,128)S(1)} custom-call(f32[1,128,128]{2,1,0:T(8,128)S(1)} %get-tuple-element.35), custom_call_target="InvertDiagBlocksLowerTriangular" | custom-call | tf_op jit(solution)/shard_map/jit(cholesky)/cholesky | solution.py:22
  396.4 0.3 convolution_dynamic-update-slice_fusion
  396.7 0.4 convolution_subtract_fusion.1
  397.1 11.7 %cholesky.238 = f32[128,128]{1,0:T(8,128)S(1)} custom-call(f32[128,128]{1,0:T(8,128)S(1)} %cholesky.275), custom_call_target="Cholesky" | custom-call | tf_op jit(solution)/shard_map/jit(cholesky)/cholesky | solution.py:22
  408.9 0.7 compare_reduce_fusion.1
  409.6 10.0 %custom-call.32 = f32[1,128,128]{1,2,0:T(8,128)S(1)} custom-call(f32[1,128,128]{2,1,0:T(8,128)S(1)} %get-tuple-element.32), custom_call_target="InvertDiagBlocksLowerTriangular" | custom-call | tf_op jit(solution)/shard_map/jit(cholesky)/cholesky | solution.py:22
  419.6 0.2 convolution_dynamic-update-slice_fusion.1
  419.8 0.4 convolution_subtract_fusion.5
  420.2 11.7 %cholesky.255 = f32[128,128]{1,0:T(8,128)S(1)} custom-call(f32[128,128]{1,0:T(8,128)S(1)} %convolution_subtract_fusion.5), custom_call_target="Cholesky" | custom-call | tf_op jit(solution)/shard_map/jit(cholesky)/cholesky | solution.py:22
  431.9 0.6 compare_reduce_fusion
  432.6 0.7 compare_reduce_fusion.2
  435.8 0.1 select_select_fusion
  435.9 10.6 %while.1 = (s32[]{:T(128)}, f32[512,512]{1,0:T(8,128)S(1)}, s32[4,2]{0,1:T(2,128)S(1)}, f32[4,128,128]{2,1,0:T(8,128)}, s32[]{:T(128)}) while((s32[]{:T(128)}, f32[512,512]{1,0:T(8,128)S(1)}, s32[4,2]{0,1:T(2,128)S(1)}, f32[4,128,128]{2,1,0:T(8,128)}, s32[]{:T(128)}) %tuple.27), condition=%wide.while_cond, body=%wide.while_body.sunk | while | flops 2 | bytes 132705 | solution.py:23
  435.9 0.1 constant_dynamic-slice_fusion.2
  436.0 0.6 fusion.70
  436.6 2.0 bitcast_dynamic-update-slice_fusion.2
  438.6 0.1 constant_dynamic-slice_fusion.2
  438.7 0.6 fusion.70
  439.3 2.0 bitcast_dynamic-update-slice_fusion.2
  441.2 0.1 constant_dynamic-slice_fusion.2
  441.3 0.6 fusion.70
  441.9 2.0 bitcast_dynamic-update-slice_fusion.2
  443.9 0.1 constant_dynamic-slice_fusion.2
  443.9 0.6 fusion.70
  444.5 2.0 bitcast_dynamic-update-slice_fusion.2
  446.5 40.1 %custom-call.33 = f32[4,128,128]{1,2,0:T(8,128)S(1)} custom-call(f32[4,128,128]{2,1,0:T(8,128)} %get-tuple-element.12), custom_call_target="InvertDiagBlocksLowerTriangular" | custom-call | tf_op jit(solution)/shard_map/triangular_solve | solution.py:23
  486.6 0.3 fusion.48
  486.9 0.2 convolution_subtract_fusion.3
  487.2 0.3 fusion.47
  487.4 0.3 convolution_subtract_fusion.2
  487.7 0.3 fusion.45
  488.0 0.3 convolution_subtract_fusion.4
  488.3 0.3 fusion.44
  488.6 0.7 pad_maximum_fusion
  (13 shorter events, 0.2 us)
Async XLA Ops:
  6.5 3.1 copy-start
  6.5 131.1 %all-reduce.11.cloned.1.call-start = ((), (), s32[]{:S(2)}) async-start(), calls=%async_computation.2 | async-start | bytes 6291456 | tf_op jit(solution)/shard_map/psum | solution.py:14
  13.6 196.1 %all-reduce.9.cloned.1.call-start = ((), (), s32[]{:S(2)}) async-start(), calls=%async_computation.1 | async-start | bytes 6291456 | tf_op jit(solution)/shard_map/psum | solution.py:14
  137.6 211.9 %all-reduce.7.cloned.1.call-start = ((), (), s32[]{:S(2)}) async-start(), calls=%async_computation | async-start | bytes 2097152 | tf_op jit(solution)/shard_map/psum | solution.py:21
  209.7 3.1 copy-start.3
  212.8 1.9 copy-start.2
  350.9 1.2 copy-start.1
Sparse Core Ops, SparseCore 0:
  13.8 123.8 all-reduce.10
  141.2 68.4 all-reduce.8
  218.7 130.8 all-reduce.6

commit v2 on v0

--- a/solution.py
+++ b/solution.py
@@ -18,7 +18,7 @@
         project = summed[index] / npw_total
         predicted = predicted + weights[index] * jnp.dot(project, history[index], precision=precise)
     local_gram = jnp.einsum("ip,jp->ij", predicted, predicted, precision=precise)
-    gram = lax.psum(local_gram, ("row", "col"))
+    gram = jnp.sum(lax.all_gather(local_gram, ("row", "col")), axis=0)
     factor = jnp.linalg.cholesky(gram / npw_total)
     return lax.linalg.triangular_solve(factor, predicted, left_side=True, lower=True)
 

time: 444 us -> 517 us (1.16)
  waiting for transfers between devices: 271 us -> 335 us
  other arithmetic: 121 us -> 132 us
    all_gather x0 -> x1, waiting for transfers between devices: none -> 194 us  [on_device(): gram = jnp.sum(lax.all_gather(local_gram, ('row', 'col')), axis=0)]
    psum x1 -> x0, waiting for transfers between devices: 130 us -> none  [on_device(): gram = lax.psum(local_gram, ('row', 'col'))]
    reduce_sum x0 -> x1, other arithmetic: none -> 12.4 us  [on_device(): gram = jnp.sum(lax.all_gather(local_gram, ('row', 'col')), axis=0)]
where the time goes in v2:
time: 517 us
  waiting for transfers between devices  335 us (65%)
  other arithmetic  132 us (26%)
  matrix products  21.5 us (4%)
  between operations  16.1 us (3%)
  local copies, waits for them, and re-layouts  11.1 us (2%)
    all_gather x1, waiting for transfers between devices, on_device(): gram = jnp.sum(lax.all_gather(local_gram, ('row', 'col')), axis=0)  194 us
    psum x1, waiting for transfers between devices, on_device(): summed = lax.psum(local_terms, ('row', 'col'))  142 us
    another operation x14, other arithmetic, on_device(): factor = jnp.linalg.cholesky(gram / npw_total)  78.7 us
    another operation x4, other arithmetic, on_device(): lax.linalg.triangular_solve(factor, predicted, left_side=True, lower=True)  41 us
    reduce_sum x1, other arithmetic, on_device(): gram = jnp.sum(lax.all_gather(local_gram, ('row', 'col')), axis=0)  12.4 us
    another operation x12, local copies, waits for them, and re-layouts  10.6 us
  transfers between devices with their start and end apart: 2, of which 2 were waited for; matrix products, arithmetic and copies ran while one was open for 0% of the time, Pallas kernels for 0%

profile of v2, /device:TPU:0, one launch (start us, length us, event | category | flops | bytes accessed | tf_op | source)
XLA Modules:
  0.0 516.7 jit_solution(13874570034546084437)
XLA Ops:
  6.5 0.0 all-reduce.4.cloned.1.call-start
  6.5 3.0 fusion.11
  9.6 3.0 fusion.14
  12.6 3.0 fusion.19
  15.6 0.0 all-reduce.4.cloned.1.call-update
  15.6 0.0 all-gather.3.cloned.1.call-start
  15.6 141.7 %all-reduce.4.cloned.1.call-done = (f32[512,512]{1,0:T(8,128)}, f32[512,512]{1,0:T(8,128)}, f32[512,512]{1,0:T(8,128)}) async-done(((f32[512,512]{1,0:T(8,128)}, f32[512,512]{1,0:T(8,128)}, f32[512,512]{1,0:T(8,128)}), (f32[512,512]{1,0:T(8,128)}, f32[512,512]{1,0:T(8,128)}, f32[512,512]{1,0:T(8,128)})) %all-reduce.4.cloned.1.call-update) | async-done | bytes 3145744 | tf_op jit(solution)/shard_map/psum | solution.py:14
  157.3 2.3 convolution_multiply_fusion.2
  159.6 2.3 fusion.1
  161.8 2.3 fusion
  164.1 2.0 fusion.61
  166.1 0.0 all-gather.3.cloned.1.call-update
  166.1 193.6 %all-gather.3.cloned.1.call-done = f32[16384,512]{1,0:T(8,128)} async-done(((f32[512,512]{1,0:T(8,128)}), f32[16384,512]{1,0:T(8,128)}) %all-gather.3.cloned.1.call-update) | async-done | bytes 33554448 | tf_op jit(solution)/shard_map/all_gather | solution.py:21
  359.7 12.4 %reduce_sum.11 = f32[512,512]{1,0:T(8,128)S(1)} reduce(f32[32,512,512]{2,1,0:T(8,128)} %bitcast.70, f32[]{:T(128)} %constant.149.clone.1), dimensions={0}, to_apply=%region_3.0 | reduce | flops 8126464 | bytes 34603012 | tf_op jit(solution)/shard_map/reduce_sum | solution.py:21
  372.2 0.3 copy.3
  372.5 0.2 fusion.2
  372.8 11.7 %cholesky.104 = f32[128,128]{1,0:T(8,128)S(1)} custom-call(f32[128,128]{1,0:T(8,128)S(1)} %cholesky.266), custom_call_target="Cholesky" | custom-call | tf_op jit(solution)/shard_map/jit(cholesky)/cholesky | solution.py:22
  384.5 0.1 cholesky.224
  384.7 9.8 %custom-call.30 = f32[1,128,128]{1,2,0:T(8,128)S(1)} custom-call(f32[1,128,128]{2,1,0:T(8,128)S(1)} %get-tuple-element.35), custom_call_target="InvertDiagBlocksLowerTriangular" | custom-call | tf_op jit(solution)/shard_map/jit(cholesky)/cholesky | solution.py:22
  394.5 0.3 constant_dynamic-update-slice_fusion.3
  394.8 0.3 convolution_subtract_fusion
  395.2 11.7 %cholesky.217 = f32[128,128]{1,0:T(8,128)S(1)} custom-call(f32[128,128]{1,0:T(8,128)S(1)} %cholesky.270), custom_call_target="Cholesky" | custom-call | tf_op jit(solution)/shard_map/jit(cholesky)/cholesky | solution.py:22
  406.9 10.0 %custom-call.31 = f32[1,128,128]{1,2,0:T(8,128)S(1)} custom-call(f32[1,128,128]{2,1,0:T(8,128)S(1)} %get-tuple-element.32), custom_call_target="InvertDiagBlocksLowerTriangular" | custom-call | tf_op jit(solution)/shard_map/jit(cholesky)/cholesky | solution.py:22
  416.9 0.3 convolution_dynamic-update-slice_fusion
  417.2 0.4 convolution_subtract_fusion.1
  417.6 11.7 %cholesky.238 = f32[128,128]{1,0:T(8,128)S(1)} custom-call(f32[128,128]{1,0:T(8,128)S(1)} %cholesky.275), custom_call_target="Cholesky" | custom-call | tf_op jit(solution)/shard_map/jit(cholesky)/cholesky | solution.py:22
  429.3 0.7 compare_reduce_fusion.1
  430.0 9.8 %custom-call.32 = f32[1,128,128]{1,2,0:T(8,128)S(1)} custom-call(f32[1,128,128]{2,1,0:T(8,128)S(1)} %get-tuple-element.29), custom_call_target="InvertDiagBlocksLowerTriangular" | custom-call | tf_op jit(solution)/shard_map/jit(cholesky)/cholesky | solution.py:22
  439.9 0.2 convolution_dynamic-update-slice_fusion.1
  440.1 0.4 convolution_subtract_fusion.5
  440.5 11.7 %cholesky.255 = f32[128,128]{1,0:T(8,128)S(1)} custom-call(f32[128,128]{1,0:T(8,128)S(1)} %convolution_subtract_fusion.5), custom_call_target="Cholesky" | custom-call | tf_op jit(solution)/shard_map/jit(cholesky)/cholesky | solution.py:22
  452.2 0.6 compare_reduce_fusion
  452.8 0.7 compare_reduce_fusion.2
  456.1 0.1 select_select_fusion
  456.2 10.9 %while.1 = (s32[]{:T(128)}, f32[512,512]{1,0:T(8,128)S(1)}, s32[4,2]{0,1:T(2,128)S(1)}, f32[4,128,128]{2,1,0:T(8,128)}, s32[]{:T(128)}) while((s32[]{:T(128)}, f32[512,512]{1,0:T(8,128)S(1)}, s32[4,2]{0,1:T(2,128)S(1)}, f32[4,128,128]{2,1,0:T(8,128)}, s32[]{:T(128)}) %tuple.27), condition=%wide.while_cond, body=%wide.while_body.sunk | while | flops 2 | bytes 132705 | solution.py:23
  456.5 0.1 constant_dynamic-slice_fusion.2
  456.6 0.6 fusion.70
  457.2 2.0 bitcast_dynamic-update-slice_fusion.2
  459.1 0.1 constant_dynamic-slice_fusion.2
  459.2 0.6 fusion.70
  459.8 2.0 bitcast_dynamic-update-slice_fusion.2
  461.8 0.1 constant_dynamic-slice_fusion.2
  461.9 0.6 fusion.70
  462.5 2.0 bitcast_dynamic-update-slice_fusion.2
  464.4 0.1 constant_dynamic-slice_fusion.2
  464.5 0.6 fusion.70
  465.1 2.0 bitcast_dynamic-update-slice_fusion.2
  467.1 40.1 %custom-call.33 = f32[4,128,128]{1,2,0:T(8,128)S(1)} custom-call(f32[4,128,128]{2,1,0:T(8,128)} %get-tuple-element.12), custom_call_target="InvertDiagBlocksLowerTriangular" | custom-call | tf_op jit(solution)/shard_map/triangular_solve | solution.py:23
  507.2 0.3 fusion.48
  507.5 0.2 convolution_subtract_fusion.3
  507.7 0.3 fusion.47
  508.0 0.3 convolution_subtract_fusion.2
  508.3 0.3 fusion.45
  508.6 0.3 convolution_subtract_fusion.4
  508.9 0.3 fusion.44
  509.2 0.7 pad_maximum_fusion
  (10 shorter events, 0.2 us)
Async XLA Ops:
  6.5 150.8 %all-reduce.4.cloned.1.call-start = ((), (), s32[]{:S(2)}) async-start(), calls=%async_computation.1 | async-start | bytes 6291456 | tf_op jit(solution)/shard_map/psum | solution.py:14
  15.6 344.2 %all-gather.3.cloned.1.call-start = ((), (), s32[]{:S(2)}) async-start(), calls=%async_computation | async-start | bytes 34603008 | tf_op jit(solution)/shard_map/all_gather | solution.py:21
Sparse Core Ops, SparseCore 0:
  15.7 141.5 all-reduce.3
  166.2 193.4 all-gather.2
